TPU v7x, 256 devices: a whole 4x4x8 slice. The times are simulated.
256 devices in a mesh: act: 64 (over x, z, core), rep: 4 (over y).
Axes of the slice: x: 4, y: 4, z: 8, core: 2. Of those that a mesh axis runs over, the one named last changes fastest.
Arguments:
- estimated_returns: float32 [512, 131072], P('act', 'rep'), may hold values from -1000 to 1000
- chosen_move_ids: int32 [512, 131072], P('act', 'rep'), may hold values from 0 to 17
- previous_eta: float32 [1], replicated, may hold values from 0.3 to 3
- trust_region_epsilon: float32 [1], replicated, may hold values from 0.02 to 1
Outputs:
- sample_importance: float32 [512, 131072], P('act', 'rep')
- goal_distribution: float32 [18, 131072], P(None, ('rep', 'act'))
- new_temperature: float32 [1], replicated
All inputs are finite; a program needn't handle non-finite values.
Results may differ from a plain program's by a relative error of at most 0.0003.
Values sent between devices are 32-bit elements; how exact they have to be, the bound alone decides.
No kernel may reach another device: no remote copies, remote signals or barrier semaphores. Data moves between devices by JAX's collectives and lax.ppermute only.
A program may use at most 64 MiB of HBM per device.

v0:
```python
import functools
import jax
import jax.numpy as jnp
from jax import lax
from jax.experimental import pallas as pl
from jax.experimental.pallas import tpu as pltpu
from jax.sharding import Mesh
from jax.sharding import PartitionSpec as P

NACT = 18
ITERS = 3
LANES = 128
LOG2E = 1.4426950408889634
ACT = ("x", "z", "core")
ALL = ("rep", "x", "z", "core")
CHIPS = ("rep", "x", "z")
PLANE = ("x", "z")
VMEM = pl.BlockSpec(memory_space=pltpu.VMEM)
SMEM = pl.BlockSpec(memory_space=pltpu.SMEM)
PARAMS = pltpu.CompilerParams(vmem_limit_bytes=8 * 1024 * 1024)


def call(body, out_shape, n_smem, n_vmem, flops=1_000_000):
    n_out = len(out_shape) if isinstance(out_shape, (tuple, list)) else None
    return pl.pallas_call(
        body,
        out_shape=out_shape,
        in_specs=[SMEM] * n_smem + [VMEM] * n_vmem,
        out_specs=VMEM if n_out is None else [VMEM] * n_out,
        compiler_params=PARAMS,
        cost_estimate=pl.CostEstimate(flops=flops, bytes_accessed=2_000_000, transcendentals=262_144),
    )


def partial_sums(q_ref, top, eta, samples):
    blocks, rows, states = q_ref.shape
    inverse = jnp.broadcast_to((1.0 / eta)[:, :1], (rows, states))
    rate = inverse * LOG2E
    top_rows = jnp.broadcast_to(top, (rows, states))

    def step(i, sums):
        z, c1, c2 = sums
        shifted = q_ref[i] - top_rows
        expo = jnp.exp2(shifted * rate)
        first = expo * shifted
        return z + expo, c1 + first, c2 + first * shifted

    zero = jnp.zeros((rows, states), jnp.float32)
    z, c1, c2 = lax.fori_loop(0, blocks, step, (zero, zero, zero), unroll=8)
    z, c1, c2 = (jnp.sum(v, axis=0, keepdims=True) for v in (z, c1, c2))
    mean = c1 / z
    kl = mean * inverse[:1] - jnp.log(z) + jnp.log(jnp.float32(samples))
    spread = c2 / z - mean * mean
    lane = lax.broadcasted_iota(jnp.int32, (1, LANES), 1)
    kl_sum = jnp.sum(kl, axis=1, keepdims=True)
    spread_sum = jnp.sum(spread, axis=1, keepdims=True)
    return jnp.where(lane == 0, kl_sum, jnp.where(lane == 1, spread_sum, 0.0))


def next_eta(gathered_ref, eta, eps, states):
    total = jnp.sum(gathered_ref[...], axis=0, keepdims=True) * jnp.float32(1.0 / states)
    divergence = jnp.broadcast_to(total[:, 0:1], eta.shape)
    deviation = jnp.broadcast_to(total[:, 1:2], eta.shape)
    change = (eps - divergence) * eta / (1.0 + deviation / eta)
    return eta * jnp.exp(-jnp.tanh(change))


def row(scalar):
    return jnp.full((1, LANES), scalar, jnp.float32)


def first_body(samples, eta_ref, eps_ref, q_ref, top_ref, eta_out, eps_out, part_ref):
    top8 = q_ref[0]
    top8 = lax.fori_loop(1, q_ref.shape[0], lambda i, m: jnp.maximum(m, q_ref[i]), top8)
    top = jnp.max(top8, axis=0, keepdims=True)
    top_ref[...] = top
    eta = row(eta_ref[0])
    eta_out[...] = eta
    eps_out[...] = row(eps_ref[0])
    part_ref[...] = partial_sums(q_ref, top, eta, samples)


def step_body(samples, states, eps_ref, q_ref, top_ref, eta_ref, gathered_ref, eta_out, part_ref):
    eta = next_eta(gathered_ref, eta_ref[...], eps_ref[...], states)
    eta_out[...] = eta
    part_ref[...] = partial_sums(q_ref, top_ref[...], eta, samples)


def last_body(samples, states, eps_ref, q_ref, top_ref, eta_ref, gathered_ref, eta_out, final_ref, back_ref):
    eta = next_eta(gathered_ref, eta_ref[...], eps_ref[...], states)
    eta_out[...] = eta
    blocks, rows, width = q_ref.shape
    rate = jnp.broadcast_to((LOG2E / eta)[:, :1], (rows, width))
    top = top_ref[...]
    top_rows = jnp.broadcast_to(top, (rows, width))
    z = lax.fori_loop(
        0, blocks, lambda i, z: z + jnp.exp2((q_ref[i] - top_rows) * rate),
        jnp.zeros((rows, width), jnp.float32), unroll=8)
    scale = jnp.float32(samples) / jnp.sum(z, axis=0, keepdims=True)
    tiles = [v[:, t : t + LANES] for v in (top, scale) for t in range(0, width, LANES)]
    tiles = jnp.concatenate(tiles, axis=0)
    back_ref[...] = jnp.broadcast_to(tiles[None], back_ref.shape)
    final_ref[0] = tiles
    final_ref[1] = jnp.broadcast_to(eta, tiles.shape)


def split_body(at_ref, ids_ref, from_core_ref, *out_refs):
    z, core = at_ref[1], at_ref[2]
    hops = len(out_refs)
    for k, out_ref in enumerate(out_refs):
        to = lax.rem(z + k, hops)
        for x in range(out_ref.shape[1]):
            out_ref[0, x] = ids_ref[x, to, core]
            out_ref[1, x] = from_core_ref[x, to]


def merge_body(at_ref, _, *refs):
    hops = len(refs) * 2 // 3
    in_refs, out_refs = refs[:hops], refs[hops:]
    for j, out_ref in enumerate(out_refs):
        to = lax.rem(at_ref[0] + j, len(out_refs))
        for k, in_ref in enumerate(in_refs):
            out_ref[k] = in_ref[:, to]


def goal_body(samples, at_ref, q_ref, final_ref, *refs):
    ids_refs, goal_ref = refs[:-1], refs[-1]
    across, along, cores = len(ids_refs), ids_refs[0].shape[0], ids_refs[0].shape[1]
    _, rows, width = q_ref.shape
    rate = LOG2E / final_ref[1]
    x, z, core = at_ref[0], at_ref[1], at_ref[2]
    for tile in range(width // LANES):
        at = slice(tile * LANES, (tile + 1) * LANES)
        top_rows = jnp.broadcast_to(final_ref[0, tile : tile + 1], (rows, LANES))
        tiles = width // LANES
        scale = final_ref[0, tiles + tile : tiles + tile + 1] * jnp.float32(1.0 / samples)
        sums = (jnp.zeros((rows, LANES), jnp.float32),) * NACT
        for j, ids_ref in enumerate(ids_refs):
            from_x = lax.rem(x + across - j , across)

            def step(k, sums):
                from_z = lax.rem(z + along - k , along)
                for c in range(cores):
                    from_core = core if c == 0 else 1 - core
                    holder = (from_x * along + from_z) * cores + from_core
                    expo = jnp.exp2((q_ref[holder, :, at] - top_rows) * rate)
                    ids = ids_ref[k, c, :, at]
                    sums = tuple(s + jnp.where(ids == n, expo, 0.0) for n, s in enumerate(sums))
                return sums

            sums = lax.fori_loop(0, along, step, sums, unroll=2)
        for n, s in enumerate(sums):
            goal_ref[n : n + 1, at] = jnp.sum(s, axis=0, keepdims=True) * scale


def weights_body(steps, at_ref, final_ref, x_ref, same_ref, other_ref, out_ref, held, sems):
    rows, width = x_ref.shape
    chips, both, _ = same_ref.shape
    tiles = both // 2
    rate = LOG2E / final_ref[1]
    core = at_ref[2]
    copies = []
    for step in range(steps):
        for chip in range(step * chips // steps, (step + 1) * chips // steps):
            for from_ref, owner in ((same_ref, chip * 2 + core), (other_ref, chip * 2 + 1 - core)):
                for t in range(tiles):
                    at = pl.ds(pl.multiple_of((owner * tiles + t) * LANES, LANES), LANES)
                    top = jnp.broadcast_to(from_ref[chip, t : t + 1], (rows, LANES))
                    scale = jnp.broadcast_to(from_ref[chip, tiles + t : tiles + t + 1], (rows, LANES))
                    held[:, at] = jnp.exp2((x_ref[:, at] - top) * rate) * scale
        part = pl.ds(step * width // steps, width // steps)
        copies.append(pltpu.make_async_copy(held.at[:, part], out_ref.at[:, part], sems.at[step]))
        copies[-1].start()
    for copy in copies:
        copy.wait()


def turned(axes):
    order = [0]
    for size in (lax.axis_size(a) for a in axes):
        turn = (2 if len(order) == 1 else 1) if axes[0] == "rep" else 0
        order = [n * size + (i + turn) % size for n in order for i in range(size)]
    return order


def send(blocks, axes):
    return lax.all_to_all(
        blocks, axes, split_axis=0, concat_axis=0, tiled=True, axis_index_groups=[turned(axes)]
    )


def shifted_by(v, axis, hops):
    size = lax.axis_size(axis)
    return lax.ppermute(v, axis, [(i, (i + hops) % size) for i in range(size)])


def on_device(estimated_returns, chosen_move_ids, previous_eta, trust_region_epsilon):
    across, along, cores = (lax.axis_size(a) for a in ACT)
    peers = lax.axis_size(ACT)
    everyone = peers * lax.axis_size("rep")
    rows, width = estimated_returns.shape
    own = width // peers
    samples, states = rows * peers, width * lax.axis_size("rep")
    f32, i32 = jnp.float32, jnp.int32
    shape = jax.ShapeDtypeStruct
    at = jnp.stack([lax.axis_index(a) for a in ACT])

    def by_owner(v):
        return v.reshape(rows, peers, own).transpose(1, 0, 2)

    q = send(by_owner(estimated_returns), ACT)

    moves = by_owner(chosen_move_ids).reshape(across, along, cores, rows, own)
    give = lax.dynamic_index_in_dim(moves, 1 - at[2], 2, keepdims=False)
    from_core = shifted_by(give, "core", 1)
    chunks = call(split_body, [shape((cores, across, rows, own), i32)] * along, 1, 2)(at, moves, from_core)
    arrived = [chunks[0]]
    for k in range(1, along):
        arrived.append(shifted_by(chunks[k], "z", k))

    row_shape = shape((1, LANES), f32)

    def sums_of_chips(part):
        chip = part + shifted_by(part, "core", 1)
        copies = jnp.broadcast_to(chip[None], (everyone // cores, 1, LANES))
        return send(copies, CHIPS).reshape(everyone // cores, LANES)

    top, eta, eps, part = call(
        functools.partial(first_body, samples), [shape((1, own), f32), row_shape, row_shape, row_shape], 2, 1
    )(previous_eta, trust_region_epsilon, q)
    for i in range(ITERS - 1):
        gathered = sums_of_chips(part)
        eta, part = call(
            functools.partial(step_body, samples, states), [row_shape, row_shape], 0, 5
        )(eps, q, top, eta, gathered)
        if i == 1:
            chunks = call(merge_body, [shape((along, cores, rows, own), i32)] * across, 1, 1 + along)(at, eta, *arrived)
            ids = [chunks[0]]
            for j in range(1, across):
                ids.append(shifted_by(chunks[j], "x", j))
    gathered = sums_of_chips(part)
    eta, final, back = call(
        functools.partial(last_body, samples, states),
        [row_shape, shape((2, 2 * own // LANES, LANES), f32), shape((peers // cores, 2 * own // LANES, LANES), f32)], 0, 5,
    )(eps, q, top, eta, gathered)
    from_same = send(back, PLANE)
    from_other = shifted_by(from_same, "core", 1)
    goal = call(
        functools.partial(goal_body, samples), shape((NACT, own), f32), 1, 2 + across, flops=20_000_000
    )(at, q, final, *ids)

    steps = 4
    weights_kernel = pl.pallas_call(
        functools.partial(weights_body, steps),
        out_shape=shape((rows, width), f32),
        in_specs=[SMEM] + [VMEM] * 4,
        out_specs=pl.BlockSpec(memory_space=pl.ANY),
        scratch_shapes=[pltpu.VMEM((rows, width), f32), pltpu.SemaphoreType.DMA((steps,))],
        compiler_params=PARAMS,
        cost_estimate=pl.CostEstimate(flops=1_000_000, bytes_accessed=2_000_000, transcendentals=262_144),
        name="weights",
    )
    weights = weights_kernel(at, final, estimated_returns, from_same, from_other)
    return weights, goal, eta[0, :1]


def solution(mesh):
    split = Mesh(mesh.devices.reshape(4, 8, 2, mesh.shape["rep"]), (*ACT, "rep"))
    placed = (P(ACT, "rep"), P(ACT, "rep"), P(), P())
    return jax.shard_map(
        on_device,
        mesh=split,
        in_specs=placed,
        out_specs=(P(ACT, "rep"), P(None, ALL), P()),
        check_vma=False,
    )
```

profile of v0, /device:TPU:64, one launch (start us, length us, event | category | flops | bytes accessed | tf_op | source)
XLA Modules:
  0.0 149.4 jit_solution(3910065942558362700)
XLA Ops:
  0.6 11.1 %all-to-all-start = ((f32[64,8,512]{2,1,0:T(8,128)}), f32[64,8,512]{2,1,0:T(8,128)S(1)}, u32[]{:S(2)}, u32[]{:S(2)}) async-start(f32[64,8,512]{2,1,0:T(8,128)} %bitcast.24), calls=%async_computation | async-start | bytes 2097152 | tf_op jit(solution)/shard_map/all_to_all | solution.py:187
  13.2 26.1 %all-to-all-done.q_ref = f32[64,8,512]{2,1,0:T(8,128)S(1)} async-done(((f32[64,8,512]{2,1,0:T(8,128)}), f32[64,8,512]{2,1,0:T(8,128)S(1)}, u32[]{:S(2)}, u32[]{:S(2)}) %all-to-all-start) | async-done | bytes 1048608 | tf_op jit(solution)/shard_map/all_to_all | solution.py:187
  39.3 0.8 shard_map.67
  40.1 1.1 collective-permute-done
  41.9 11.6 %all-to-all-start.1 = ((f32[128,1,128]{2,1,0:T(1,128)}), f32[128,1,128]{2,1,0:T(1,128)S(1)}, u32[]{:S(2)}, u32[]{:S(2)}) async-start(f32[128,1,128]{2,1,0:T(1,128)} %broadcast_in_dim.25), calls=%async_computation.1 | async-start | bytes 131072 | tf_op jit(solution)/shard_map/all_to_all | solution.py:187
  53.7 8.1 %all-to-all-done.1 = f32[128,1,128]{2,1,0:T(1,128)S(1)} async-done(((f32[128,1,128]{2,1,0:T(1,128)}), f32[128,1,128]{2,1,0:T(1,128)S(1)}, u32[]{:S(2)}, u32[]{:S(2)}) %all-to-all-start.1) | async-done | bytes 65568 | tf_op jit(solution)/shard_map/all_to_all | solution.py:187
  62.4 1.2 collective-permute-done.1
  64.2 9.1 %all-to-all-start.2 = ((f32[128,1,128]{2,1,0:T(1,128)}), f32[128,1,128]{2,1,0:T(1,128)S(1)}, u32[]{:S(2)}, u32[]{:S(2)}) async-start(f32[128,1,128]{2,1,0:T(1,128)} %broadcast_in_dim.27), calls=%async_computation.2 | async-start | bytes 131072 | tf_op jit(solution)/shard_map/all_to_all | solution.py:187
  73.4 8.2 %all-to-all-done.2 = f32[128,1,128]{2,1,0:T(1,128)S(1)} async-done(((f32[128,1,128]{2,1,0:T(1,128)}), f32[128,1,128]{2,1,0:T(1,128)S(1)}, u32[]{:S(2)}, u32[]{:S(2)}) %all-to-all-start.2) | async-done | bytes 65568 | tf_op jit(solution)/shard_map/all_to_all | solution.py:187
  82.3 1.3 shard_map.71
  83.6 1.1 collective-permute-start.10
  86.1 11.9 %all-to-all-start.3 = ((f32[128,1,128]{2,1,0:T(1,128)}), f32[128,1,128]{2,1,0:T(1,128)S(1)}, u32[]{:S(2)}, u32[]{:S(2)}) async-start(f32[128,1,128]{2,1,0:T(1,128)} %broadcast_in_dim.29), calls=%async_computation.3 | async-start | bytes 131072 | tf_op jit(solution)/shard_map/all_to_all | solution.py:187
  98.0 1.5 %collective-permute-start.5 = (s32[2,4,8,512]{3,2,1,0:T(8,128)S(1)}, s32[2,4,8,512]{3,2,1,0:T(8,128)S(1)}, u32[]{:S(2)}, u32[]{:S(2)}) collective-permute-start(s32[2,4,8,512]{3,2,1,0:T(8,128)S(1)} %get-tuple-element.37), channel_id=1, source_target_pairs={{0,8},{8,16},{16,24},{24,32},{32,40},{40,48},{48,56},{56,0},{1,9},... | collective-permute-start | bytes 393224 | tf_op jit(solution)/shard_map/ppermute | solution.py:194
  99.5 3.6 %collective-permute-start.6 = (s32[2,4,8,512]{3,2,1,0:T(8,128)S(1)}, s32[2,4,8,512]{3,2,1,0:T(8,128)S(1)}, u32[]{:S(2)}, u32[]{:S(2)}) collective-permute-start(s32[2,4,8,512]{3,2,1,0:T(8,128)S(1)} %get-tuple-element.38), channel_id=1, source_target_pairs={{0,16},{8,24},{16,32},{24,40},{32,48},{40,56},{48,0},{56,8},{1,17}... | collective-permute-start | bytes 393224 | tf_op jit(solution)/shard_map/ppermute | solution.py:194
  103.7 4.4 %collective-permute-start.8 = (s32[2,4,8,512]{3,2,1,0:T(8,128)S(1)}, s32[2,4,8,512]{3,2,1,0:T(8,128)S(1)}, u32[]{:S(2)}, u32[]{:S(2)}) collective-permute-start(s32[2,4,8,512]{3,2,1,0:T(8,128)S(1)} %get-tuple-element.40), channel_id=1, source_target_pairs={{0,32},{8,40},{16,48},{24,56},{32,0},{40,8},{48,16},{56,24},{1,33}... | collective-permute-start | bytes 393224 | tf_op jit(solution)/shard_map/ppermute | solution.py:194
  108.7 1.1 shard_map.70
  109.8 9.4 %all-to-all-start.4 = ((f32[32,8,128]{2,1,0:T(8,128)}), f32[32,8,128]{2,1,0:T(8,128)S(1)}, u32[]{:S(2)}, u32[]{:S(2)}) async-start(f32[32,8,128]{2,1,0:T(8,128)} %get-tuple-element.35), calls=%async_computation.4 | async-start | bytes 262144 | tf_op jit(solution)/shard_map/all_to_all | solution.py:187
  119.3 1.5 collective-permute-done.7.refs_3_
  120.7 7.9 %collective-permute-done.8.refs_4_ = s32[2,4,8,512]{3,2,1,0:T(8,128)S(1)} collective-permute-done((s32[2,4,8,512]{3,2,1,0:T(8,128)S(1)}, s32[2,4,8,512]{3,2,1,0:T(8,128)S(1)}, u32[]{:S(2)}, u32[]{:S(2)}) %collective-permute-start.8) | collective-permute-done | bytes 131104 | tf_op jit(solution)/shard_map/ppermute | solution.py:194
  129.7 3.8 %collective-permute-start.13 = (s32[8,2,8,512]{3,2,1,0:T(8,128)S(1)}, s32[8,2,8,512]{3,2,1,0:T(8,128)S(1)}, u32[]{:S(2)}, u32[]{:S(2)}) collective-permute-start(s32[8,2,8,512]{3,2,1,0:T(8,128)S(1)} %get-tuple-element.46), channel_id=1, source_target_pairs={{0,128},{64,192},{128,0},{192,64},{1,129},{65,193},{129,1},{193,65... | collective-permute-start | bytes 786440 | tf_op jit(solution)/shard_map/ppermute | solution.py:194
  133.9 5.1 %collective-permute-done.12.refs_1_ = s32[8,2,8,512]{3,2,1,0:T(8,128)S(1)} collective-permute-done((s32[8,2,8,512]{3,2,1,0:T(8,128)S(1)}, s32[8,2,8,512]{3,2,1,0:T(8,128)S(1)}, u32[]{:S(2)}, u32[]{:S(2)}) %collective-permute-start.12) | collective-permute-done | bytes 262176 | tf_op jit(solution)/shard_map/ppermute | solution.py:194
  139.0 4.4 %collective-permute-done.13.refs_2_ = s32[8,2,8,512]{3,2,1,0:T(8,128)S(1)} collective-permute-done((s32[8,2,8,512]{3,2,1,0:T(8,128)S(1)}, s32[8,2,8,512]{3,2,1,0:T(8,128)S(1)}, u32[]{:S(2)}, u32[]{:S(2)}) %collective-permute-start.13) | collective-permute-done | bytes 262176 | tf_op jit(solution)/shard_map/ppermute | solution.py:194
  143.5 4.1 %shard_map.73 = f32[18,512]{1,0:T(8,128)} custom-call(s32[3]{0:T(128)S(1)} %pad_add_fusion.at_ref, f32[64,8,512]{2,1,0:T(8,128)S(1)} %all-to-all-done.q_ref, f32[2,8,128]{2,1,0:T(8,128)S(1)} %get-tuple-element.34.final_ref, s32[8,2,8,512]{3,2,1,0:T(8,128)S(1)} %get-tuple-element.44.refs_0_, s32[8,2,8,512]{3,2,1,0:T(8,128)S(1)} %collective-permute-done.12.refs_1_, ...), custom_call_target="tpu_custom_call" | custom-call | flops 20000000 | bytes 2000000 | tf_op jit(solution)/shard_map/pallas_call | solution.py:248
  147.5 1.7 %weights.1 = f32[8,32768]{1,0:T(8,128)} custom-call(s32[3]{0:T(128)S(1)} %pad_add_fusion.at_ref, f32[2,8,128]{2,1,0:T(8,128)S(1)} %get-tuple-element.34.final_ref, f32[8,32768]{1,0:T(8,128)S(1)} %copy-done, f32[32,8,128]{2,1,0:T(8,128)S(1)} %all-to-all-done.4.same_ref, f32[32,8,128]{2,1,0:T(8,128)S(1)} %collective-permute-done.3.other_ref), custom_call_target="tpu_custom_call" | custom-call | flops 1000000 | bytes 2000000 | tf_op jit(solution)/shard_map/weights/pallas_call | solution.py:263
  (36 shorter events, 6.9 us)
Async XLA Ops:
  0.6 38.6 %all-to-all-start = ((f32[64,8,512]{2,1,0:T(8,128)}), f32[64,8,512]{2,1,0:T(8,128)S(1)}, u32[]{:S(2)}, u32[]{:S(2)}) async-start(f32[64,8,512]{2,1,0:T(8,128)} %bitcast.24), calls=%async_computation | async-start | bytes 2097152 | tf_op jit(solution)/shard_map/all_to_all | solution.py:187
  11.8 41.7 %copy-start.1 = (s32[8,32768]{1,0:T(8,128)S(1)}, s32[8,32768]{1,0:T(8,128)}, u32[]{:S(2)}) copy-start(s32[8,32768]{1,0:T(8,128)} %param.5) | copy-start | bytes 3145732
  40.0 1.2 collective-permute-start
  41.9 19.9 %all-to-all-start.1 = ((f32[128,1,128]{2,1,0:T(1,128)}), f32[128,1,128]{2,1,0:T(1,128)S(1)}, u32[]{:S(2)}, u32[]{:S(2)}) async-start(f32[128,1,128]{2,1,0:T(1,128)} %broadcast_in_dim.25), calls=%async_computation.1 | async-start | bytes 131072 | tf_op jit(solution)/shard_map/all_to_all | solution.py:187
  53.6 28.7 %collective-permute-start.4 = (s32[4,8,8,512]{3,2,1,0:T(8,128)S(1)}, s32[4,8,8,512]{3,2,1,0:T(8,128)S(1)}, u32[]{:S(2)}, u32[]{:S(2)}) collective-permute-start(s32[4,8,8,512]{3,2,1,0:T(8,128)S(1)} %dynamic-slice_bitcast_fusion), channel_id=1, source_target_pairs={{0,4},{4,0},{1,5},{5,1},{2,6},{6,2},{3,7},{7,3},{8,12},{12,8},{9,1... | collective-permute-start | bytes 1572872 | tf_op jit(solution)/shard_map/ppermute | solution.py:194
  62.4 1.2 collective-permute-start.1
  64.2 17.4 %all-to-all-start.2 = ((f32[128,1,128]{2,1,0:T(1,128)}), f32[128,1,128]{2,1,0:T(1,128)S(1)}, u32[]{:S(2)}, u32[]{:S(2)}) async-start(f32[128,1,128]{2,1,0:T(1,128)} %broadcast_in_dim.27), calls=%async_computation.2 | async-start | bytes 131072 | tf_op jit(solution)/shard_map/all_to_all | solution.py:187
  82.2 3.2 %collective-permute-start.2 = (f32[1,128]{1,0:T(1,128)S(1)}, f32[1,128]{1,0:T(1,128)S(1)}, u32[]{:S(2)}, u32[]{:S(2)}) collective-permute-start(f32[1,128]{1,0:T(1,128)S(1)} %get-tuple-element.33), channel_id=1, source_target_pairs={{0,4},{4,0},{1,5},{5,1},{2,6},{6,2},{3,7},{7,3},{8,12},{12,8},{9,1... | collective-permute-start | bytes 1544 | tf_op jit(solution)/shard_map/ppermute | solution.py:194
  83.6 20.1 %collective-permute-start.10 = (s32[2,4,8,512]{3,2,1,0:T(8,128)}, s32[2,4,8,512]{3,2,1,0:T(8,128)S(1)}, u32[]{:S(2)}, u32[]{:S(2)}) collective-permute-start(s32[2,4,8,512]{3,2,1,0:T(8,128)} %get-tuple-element.42), channel_id=1, source_target_pairs={{0,48},{8,56},{16,0},{24,8},{32,16},{40,24},{48,32},{56,40},{1,49}... | collective-permute-start | bytes 393224 | tf_op jit(solution)/shard_map/ppermute | solution.py:194
  84.7 23.5 %collective-permute-start.11 = (s32[2,4,8,512]{3,2,1,0:T(8,128)S(1)}, s32[2,4,8,512]{3,2,1,0:T(8,128)S(1)}, u32[]{:S(2)}, u32[]{:S(2)}) collective-permute-start(s32[2,4,8,512]{3,2,1,0:T(8,128)S(1)} %get-tuple-element.43), channel_id=1, source_target_pairs={{0,56},{8,0},{16,8},{24,16},{32,24},{40,32},{48,40},{56,48},{1,57}... | collective-permute-start | bytes 393224 | tf_op jit(solution)/shard_map/ppermute | solution.py:194
  86.1 22.6 %all-to-all-start.3 = ((f32[128,1,128]{2,1,0:T(1,128)}), f32[128,1,128]{2,1,0:T(1,128)S(1)}, u32[]{:S(2)}, u32[]{:S(2)}) async-start(f32[128,1,128]{2,1,0:T(1,128)} %broadcast_in_dim.29), calls=%async_computation.3 | async-start | bytes 131072 | tf_op jit(solution)/shard_map/all_to_all | solution.py:187
  98.0 21.3 %collective-permute-start.5 = (s32[2,4,8,512]{3,2,1,0:T(8,128)S(1)}, s32[2,4,8,512]{3,2,1,0:T(8,128)S(1)}, u32[]{:S(2)}, u32[]{:S(2)}) collective-permute-start(s32[2,4,8,512]{3,2,1,0:T(8,128)S(1)} %get-tuple-element.37), channel_id=1, source_target_pairs={{0,8},{8,16},{16,24},{24,32},{32,40},{40,48},{48,56},{56,0},{1,9},... | collective-permute-start | bytes 393224 | tf_op jit(solution)/shard_map/ppermute | solution.py:194
  99.5 19.7 %collective-permute-start.6 = (s32[2,4,8,512]{3,2,1,0:T(8,128)S(1)}, s32[2,4,8,512]{3,2,1,0:T(8,128)S(1)}, u32[]{:S(2)}, u32[]{:S(2)}) collective-permute-start(s32[2,4,8,512]{3,2,1,0:T(8,128)S(1)} %get-tuple-element.38), channel_id=1, source_target_pairs={{0,16},{8,24},{16,32},{24,40},{32,48},{40,56},{48,0},{56,8},{1,17}... | collective-permute-start | bytes 393224 | tf_op jit(solution)/shard_map/ppermute | solution.py:194
  103.1 17.6 %collective-permute-start.7 = (s32[2,4,8,512]{3,2,1,0:T(8,128)S(1)}, s32[2,4,8,512]{3,2,1,0:T(8,128)S(1)}, u32[]{:S(2)}, u32[]{:S(2)}) collective-permute-start(s32[2,4,8,512]{3,2,1,0:T(8,128)S(1)} %get-tuple-element.39), channel_id=1, source_target_pairs={{0,24},{8,32},{16,40},{24,48},{32,56},{40,0},{48,8},{56,16},{1,25}... | collective-permute-start | bytes 393224 | tf_op jit(solution)/shard_map/ppermute | solution.py:194
  103.7 24.9 %collective-permute-start.8 = (s32[2,4,8,512]{3,2,1,0:T(8,128)S(1)}, s32[2,4,8,512]{3,2,1,0:T(8,128)S(1)}, u32[]{:S(2)}, u32[]{:S(2)}) collective-permute-start(s32[2,4,8,512]{3,2,1,0:T(8,128)S(1)} %get-tuple-element.40), channel_id=1, source_target_pairs={{0,32},{8,40},{16,48},{24,56},{32,0},{40,8},{48,16},{56,24},{1,33}... | collective-permute-start | bytes 393224 | tf_op jit(solution)/shard_map/ppermute | solution.py:194
  108.2 20.5 %collective-permute-start.9 = (s32[2,4,8,512]{3,2,1,0:T(8,128)S(1)}, s32[2,4,8,512]{3,2,1,0:T(8,128)S(1)}, u32[]{:S(2)}, u32[]{:S(2)}) collective-permute-start(s32[2,4,8,512]{3,2,1,0:T(8,128)S(1)} %get-tuple-element.41), channel_id=1, source_target_pairs={{0,40},{8,48},{16,56},{24,0},{32,8},{40,16},{48,24},{56,32},{1,41}... | collective-permute-start | bytes 393224 | tf_op jit(solution)/shard_map/ppermute | solution.py:194
  109.8 24.1 %all-to-all-start.4 = ((f32[32,8,128]{2,1,0:T(8,128)}), f32[32,8,128]{2,1,0:T(8,128)S(1)}, u32[]{:S(2)}, u32[]{:S(2)}) async-start(f32[32,8,128]{2,1,0:T(8,128)} %get-tuple-element.35), calls=%async_computation.4 | async-start | bytes 262144 | tf_op jit(solution)/shard_map/all_to_all | solution.py:187
  129.3 9.7 %collective-permute-start.12 = (s32[8,2,8,512]{3,2,1,0:T(8,128)S(1)}, s32[8,2,8,512]{3,2,1,0:T(8,128)S(1)}, u32[]{:S(2)}, u32[]{:S(2)}) collective-permute-start(s32[8,2,8,512]{3,2,1,0:T(8,128)S(1)} %get-tuple-element.45), channel_id=1, source_target_pairs={{0,64},{64,128},{128,192},{192,0},{1,65},{65,129},{129,193},{193,1... | collective-permute-start | bytes 786440 | tf_op jit(solution)/shard_map/ppermute | solution.py:194
  129.7 13.8 %collective-permute-start.13 = (s32[8,2,8,512]{3,2,1,0:T(8,128)S(1)}, s32[8,2,8,512]{3,2,1,0:T(8,128)S(1)}, u32[]{:S(2)}, u32[]{:S(2)}) collective-permute-start(s32[8,2,8,512]{3,2,1,0:T(8,128)S(1)} %get-tuple-element.46), channel_id=1, source_target_pairs={{0,128},{64,192},{128,0},{192,64},{1,129},{65,193},{129,1},{193,65... | collective-permute-start | bytes 786440 | tf_op jit(solution)/shard_map/ppermute | solution.py:194
  133.4 10.0 %collective-permute-start.14 = (s32[8,2,8,512]{3,2,1,0:T(8,128)S(1)}, s32[8,2,8,512]{3,2,1,0:T(8,128)S(1)}, u32[]{:S(2)}, u32[]{:S(2)}) collective-permute-start(s32[8,2,8,512]{3,2,1,0:T(8,128)S(1)} %get-tuple-element.47), channel_id=1, source_target_pairs={{0,192},{64,0},{128,64},{192,128},{1,193},{65,1},{129,65},{193,129... | collective-permute-start | bytes 786440 | tf_op jit(solution)/shard_map/ppermute | solution.py:194
  133.9 13.7 %collective-permute-start.3 = (f32[32,8,128]{2,1,0:T(8,128)S(1)}, f32[32,8,128]{2,1,0:T(8,128)S(1)}, u32[]{:S(2)}, u32[]{:S(2)}) collective-permute-start(f32[32,8,128]{2,1,0:T(8,128)S(1)} %all-to-all-done.4.same_ref), channel_id=1, source_target_pairs={{0,4},{4,0},{1,5},{5,1},{2,6},{6,2},{3,7},{7,3},{8,12},{12,8},{9,1... | collective-permute-start | bytes 393224 | tf_op jit(solution)/shard_map/ppermute | solution.py:194
  143.5 4.1 %copy-start = (f32[8,32768]{1,0:T(8,128)S(1)}, f32[8,32768]{1,0:T(8,128)}, u32[]{:S(2)}) copy-start(f32[8,32768]{1,0:T(8,128)} %x_ref.1) | copy-start | bytes 3145732
where the time goes:
time: 150 us; the launch traced here: 149 us
  starting transfers between devices  70.5 us (47%)
  waiting for transfers between devices  63.6 us (42%)
  Pallas kernels  10.8 us (7%)
  between operations  2.31 us (2%)
  local copies, waits for them, and re-layouts  2.07 us (1%)
    all_to_all x5, starting transfers between devices, send(): lax.all_to_all(blocks, axes, split_axis=0, concat_axis=0, tiled=True, axi...  53.3 us
    all_to_all x5, waiting for transfers between devices, send(): lax.all_to_all(blocks, axes, split_axis=0, concat_axis=0, tiled=True, axi...  42.4 us
    ppermute x15, waiting for transfers between devices, shifted_by(): return lax.ppermute(v, axis, [(i, (i + hops) % size) for i in range(size)])  21.3 us
    ppermute x15, starting transfers between devices, shifted_by(): return lax.ppermute(v, axis, [(i, (i + hops) % size) for i in range(size)])  17.2 us
    pallas_call x1, Pallas kernels, on_device(): call(functools.partial(goal_body, samples), shape((NACT, own), f32), 1, 2...  4.07 us
  transfers between devices with their start and end apart: 20, of which 9 were waited for; matrix products, arithmetic and copies ran while one was open for 1% of the time, Pallas kernels for 6%

commit v1 on v0

--- a/solution.py
+++ b/solution.py
@@ -46,7 +46,7 @@
         return z + expo, c1 + first, c2 + first * shifted
 
     zero = jnp.zeros((rows, states), jnp.float32)
-    z, c1, c2 = lax.fori_loop(0, blocks, step, (zero, zero, zero), unroll=8)
+    z, c1, c2 = lax.fori_loop(0, blocks, step, (zero, zero, zero), unroll=16)
     z, c1, c2 = (jnp.sum(v, axis=0, keepdims=True) for v in (z, c1, c2))
     mean = c1 / z
     kl = mean * inverse[:1] - jnp.log(z) + jnp.log(jnp.float32(samples))
@@ -71,7 +71,7 @@
 
 def first_body(samples, eta_ref, eps_ref, q_ref, top_ref, eta_out, eps_out, part_ref):
     top8 = q_ref[0]
-    top8 = lax.fori_loop(1, q_ref.shape[0], lambda i, m: jnp.maximum(m, q_ref[i]), top8)
+    top8 = lax.fori_loop(1, q_ref.shape[0], lambda i, m: jnp.maximum(m, q_ref[i]), top8, unroll=9)
     top = jnp.max(top8, axis=0, keepdims=True)
     top_ref[...] = top
     eta = row(eta_ref[0])
@@ -95,7 +95,7 @@
     top_rows = jnp.broadcast_to(top, (rows, width))
     z = lax.fori_loop(
         0, blocks, lambda i, z: z + jnp.exp2((q_ref[i] - top_rows) * rate),
-        jnp.zeros((rows, width), jnp.float32), unroll=8)
+        jnp.zeros((rows, width), jnp.float32), unroll=16)
     scale = jnp.float32(samples) / jnp.sum(z, axis=0, keepdims=True)
     tiles = [v[:, t : t + LANES] for v in (top, scale) for t in range(0, width, LANES)]
     tiles = jnp.concatenate(tiles, axis=0)

time: 150 us -> 150 us (level)
  no operation moved by 1% of the time
where the time goes in v1:
time: 150 us; the launch traced here: 149 us
  starting transfers between devices  70.6 us (47%)
  waiting for transfers between devices  63.7 us (42%)
  Pallas kernels  10.5 us (7%)
  between operations  2.31 us (2%)
  local copies, waits for them, and re-layouts  2.07 us (1%)
    all_to_all x5, starting transfers between devices, send(): lax.all_to_all(blocks, axes, split_axis=0, concat_axis=0, tiled=True, axi...  53.3 us
    all_to_all x5, waiting for transfers between devices, send(): lax.all_to_all(blocks, axes, split_axis=0, concat_axis=0, tiled=True, axi...  42.4 us
    ppermute x15, waiting for transfers between devices, shifted_by(): return lax.ppermute(v, axis, [(i, (i + hops) % size) for i in range(size)])  21.3 us
    ppermute x15, starting transfers between devices, shifted_by(): return lax.ppermute(v, axis, [(i, (i + hops) % size) for i in range(size)])  17.4 us
    pallas_call x1, Pallas kernels, on_device(): call(functools.partial(goal_body, samples), shape((NACT, own), f32), 1, 2...  4.07 us
  transfers between devices with their start and end apart: 20, of which 9 were waited for; matrix products, arithmetic and copies ran while one was open for 1% of the time, Pallas kernels for 6%

profile of v1, /device:TPU:64, one launch (start us, length us, event | category | flops | bytes accessed | tf_op | source)
XLA Modules:
  0.0 149.3 jit_solution(5400177847465193762)
XLA Ops:
  0.6 11.1 %all-to-all-start = ((f32[64,8,512]{2,1,0:T(8,128)}), f32[64,8,512]{2,1,0:T(8,128)S(1)}, u32[]{:S(2)}, u32[]{:S(2)}) async-start(f32[64,8,512]{2,1,0:T(8,128)} %bitcast.24), calls=%async_computation | async-start | bytes 2097152 | tf_op jit(solution)/shard_map/all_to_all | solution.py:187
  13.2 26.1 %all-to-all-done.q_ref = f32[64,8,512]{2,1,0:T(8,128)S(1)} async-done(((f32[64,8,512]{2,1,0:T(8,128)}), f32[64,8,512]{2,1,0:T(8,128)S(1)}, u32[]{:S(2)}, u32[]{:S(2)}) %all-to-all-start) | async-done | bytes 1048608 | tf_op jit(solution)/shard_map/all_to_all | solution.py:187
  39.8 1.1 collective-permute-done
  41.6 11.6 %all-to-all-start.1 = ((f32[128,1,128]{2,1,0:T(1,128)}), f32[128,1,128]{2,1,0:T(1,128)S(1)}, u32[]{:S(2)}, u32[]{:S(2)}) async-start(f32[128,1,128]{2,1,0:T(1,128)} %broadcast_in_dim.25), calls=%async_computation.1 | async-start | bytes 131072 | tf_op jit(solution)/shard_map/all_to_all | solution.py:187
  53.4 8.1 %all-to-all-done.1 = f32[128,1,128]{2,1,0:T(1,128)S(1)} async-done(((f32[128,1,128]{2,1,0:T(1,128)}), f32[128,1,128]{2,1,0:T(1,128)S(1)}, u32[]{:S(2)}, u32[]{:S(2)}) %all-to-all-start.1) | async-done | bytes 65568 | tf_op jit(solution)/shard_map/all_to_all | solution.py:187
  62.1 1.2 collective-permute-done.1
  64.0 9.1 %all-to-all-start.2 = ((f32[128,1,128]{2,1,0:T(1,128)}), f32[128,1,128]{2,1,0:T(1,128)S(1)}, u32[]{:S(2)}, u32[]{:S(2)}) async-start(f32[128,1,128]{2,1,0:T(1,128)} %broadcast_in_dim.27), calls=%async_computation.2 | async-start | bytes 131072 | tf_op jit(solution)/shard_map/all_to_all | solution.py:187
  73.1 8.2 %all-to-all-done.2 = f32[128,1,128]{2,1,0:T(1,128)S(1)} async-done(((f32[128,1,128]{2,1,0:T(1,128)}), f32[128,1,128]{2,1,0:T(1,128)S(1)}, u32[]{:S(2)}, u32[]{:S(2)}) %all-to-all-start.2) | async-done | bytes 65568 | tf_op jit(solution)/shard_map/all_to_all | solution.py:187
  82.0 1.3 shard_map.71
  83.3 1.1 collective-permute-start.10
  84.4 0.7 collective-permute-start.11
  85.8 11.9 %all-to-all-start.3 = ((f32[128,1,128]{2,1,0:T(1,128)}), f32[128,1,128]{2,1,0:T(1,128)S(1)}, u32[]{:S(2)}, u32[]{:S(2)}) async-start(f32[128,1,128]{2,1,0:T(1,128)} %broadcast_in_dim.29), calls=%async_computation.3 | async-start | bytes 131072 | tf_op jit(solution)/shard_map/all_to_all | solution.py:187
  97.7 1.7 %collective-permute-start.5 = (s32[2,4,8,512]{3,2,1,0:T(8,128)S(1)}, s32[2,4,8,512]{3,2,1,0:T(8,128)S(1)}, u32[]{:S(2)}, u32[]{:S(2)}) collective-permute-start(s32[2,4,8,512]{3,2,1,0:T(8,128)S(1)} %get-tuple-element.37), channel_id=1, source_target_pairs={{0,8},{8,16},{16,24},{24,32},{32,40},{40,48},{48,56},{56,0},{1,9},... | collective-permute-start | bytes 393224 | tf_op jit(solution)/shard_map/ppermute | solution.py:194
  99.4 3.6 %collective-permute-start.6 = (s32[2,4,8,512]{3,2,1,0:T(8,128)S(1)}, s32[2,4,8,512]{3,2,1,0:T(8,128)S(1)}, u32[]{:S(2)}, u32[]{:S(2)}) collective-permute-start(s32[2,4,8,512]{3,2,1,0:T(8,128)S(1)} %get-tuple-element.38), channel_id=1, source_target_pairs={{0,16},{8,24},{16,32},{24,40},{32,48},{40,56},{48,0},{56,8},{1,17}... | collective-permute-start | bytes 393224 | tf_op jit(solution)/shard_map/ppermute | solution.py:194
  103.6 4.4 %collective-permute-start.8 = (s32[2,4,8,512]{3,2,1,0:T(8,128)S(1)}, s32[2,4,8,512]{3,2,1,0:T(8,128)S(1)}, u32[]{:S(2)}, u32[]{:S(2)}) collective-permute-start(s32[2,4,8,512]{3,2,1,0:T(8,128)S(1)} %get-tuple-element.40), channel_id=1, source_target_pairs={{0,32},{8,40},{16,48},{24,56},{32,0},{40,8},{48,16},{56,24},{1,33}... | collective-permute-start | bytes 393224 | tf_op jit(solution)/shard_map/ppermute | solution.py:194
  108.6 1.0 shard_map.70
  109.7 9.4 %all-to-all-start.4 = ((f32[32,8,128]{2,1,0:T(8,128)}), f32[32,8,128]{2,1,0:T(8,128)S(1)}, u32[]{:S(2)}, u32[]{:S(2)}) async-start(f32[32,8,128]{2,1,0:T(8,128)} %get-tuple-element.35), calls=%async_computation.4 | async-start | bytes 262144 | tf_op jit(solution)/shard_map/all_to_all | solution.py:187
  119.1 1.8 %collective-permute-done.7.refs_3_ = s32[2,4,8,512]{3,2,1,0:T(8,128)S(1)} collective-permute-done((s32[2,4,8,512]{3,2,1,0:T(8,128)S(1)}, s32[2,4,8,512]{3,2,1,0:T(8,128)S(1)}, u32[]{:S(2)}, u32[]{:S(2)}) %collective-permute-start.7) | collective-permute-done | bytes 131104 | tf_op jit(solution)/shard_map/ppermute | solution.py:194
  120.9 7.6 %collective-permute-done.8.refs_4_ = s32[2,4,8,512]{3,2,1,0:T(8,128)S(1)} collective-permute-done((s32[2,4,8,512]{3,2,1,0:T(8,128)S(1)}, s32[2,4,8,512]{3,2,1,0:T(8,128)S(1)}, u32[]{:S(2)}, u32[]{:S(2)}) %collective-permute-start.8) | collective-permute-done | bytes 131104 | tf_op jit(solution)/shard_map/ppermute | solution.py:194
  129.5 3.8 %collective-permute-start.13 = (s32[8,2,8,512]{3,2,1,0:T(8,128)S(1)}, s32[8,2,8,512]{3,2,1,0:T(8,128)S(1)}, u32[]{:S(2)}, u32[]{:S(2)}) collective-permute-start(s32[8,2,8,512]{3,2,1,0:T(8,128)S(1)} %get-tuple-element.46), channel_id=1, source_target_pairs={{0,128},{64,192},{128,0},{192,64},{1,129},{65,193},{129,1},{193,65... | collective-permute-start | bytes 786440 | tf_op jit(solution)/shard_map/ppermute | solution.py:194
  133.7 5.1 %collective-permute-done.12.refs_1_ = s32[8,2,8,512]{3,2,1,0:T(8,128)S(1)} collective-permute-done((s32[8,2,8,512]{3,2,1,0:T(8,128)S(1)}, s32[8,2,8,512]{3,2,1,0:T(8,128)S(1)}, u32[]{:S(2)}, u32[]{:S(2)}) %collective-permute-start.12) | collective-permute-done | bytes 262176 | tf_op jit(solution)/shard_map/ppermute | solution.py:194
  138.8 4.6 %collective-permute-done.13.refs_2_ = s32[8,2,8,512]{3,2,1,0:T(8,128)S(1)} collective-permute-done((s32[8,2,8,512]{3,2,1,0:T(8,128)S(1)}, s32[8,2,8,512]{3,2,1,0:T(8,128)S(1)}, u32[]{:S(2)}, u32[]{:S(2)}) %collective-permute-start.13) | collective-permute-done | bytes 262176 | tf_op jit(solution)/shard_map/ppermute | solution.py:194
  143.4 4.1 %shard_map.73 = f32[18,512]{1,0:T(8,128)} custom-call(s32[3]{0:T(128)S(1)} %pad_add_fusion.at_ref, f32[64,8,512]{2,1,0:T(8,128)S(1)} %all-to-all-done.q_ref, f32[2,8,128]{2,1,0:T(8,128)S(1)} %get-tuple-element.34.final_ref, s32[8,2,8,512]{3,2,1,0:T(8,128)S(1)} %get-tuple-element.44.refs_0_, s32[8,2,8,512]{3,2,1,0:T(8,128)S(1)} %collective-permute-done.12.refs_1_, ...), custom_call_target="tpu_custom_call" | custom-call | flops 20000000 | bytes 2000000 | tf_op jit(solution)/shard_map/pallas_call | solution.py:248
  147.4 1.7 %weights.1 = f32[8,32768]{1,0:T(8,128)} custom-call(s32[3]{0:T(128)S(1)} %pad_add_fusion.at_ref, f32[2,8,128]{2,1,0:T(8,128)S(1)} %get-tuple-element.34.final_ref, f32[8,32768]{1,0:T(8,128)S(1)} %copy-done, f32[32,8,128]{2,1,0:T(8,128)S(1)} %all-to-all-done.4.same_ref, f32[32,8,128]{2,1,0:T(8,128)S(1)} %collective-permute-done.3.other_ref), custom_call_target="tpu_custom_call" | custom-call | flops 1000000 | bytes 2000000 | tf_op jit(solution)/shard_map/weights/pallas_call | solution.py:263
  (36 shorter events, 6.7 us)
Async XLA Ops:
  0.6 38.6 %all-to-all-start = ((f32[64,8,512]{2,1,0:T(8,128)}), f32[64,8,512]{2,1,0:T(8,128)S(1)}, u32[]{:S(2)}, u32[]{:S(2)}) async-start(f32[64,8,512]{2,1,0:T(8,128)} %bitcast.24), calls=%async_computation | async-start | bytes 2097152 | tf_op jit(solution)/shard_map/all_to_all | solution.py:187
  11.8 41.5 %copy-start.1 = (s32[8,32768]{1,0:T(8,128)S(1)}, s32[8,32768]{1,0:T(8,128)}, u32[]{:S(2)}) copy-start(s32[8,32768]{1,0:T(8,128)} %param.5) | copy-start | bytes 3145732
  39.8 1.2 collective-permute-start
  41.6 19.9 %all-to-all-start.1 = ((f32[128,1,128]{2,1,0:T(1,128)}), f32[128,1,128]{2,1,0:T(1,128)S(1)}, u32[]{:S(2)}, u32[]{:S(2)}) async-start(f32[128,1,128]{2,1,0:T(1,128)} %broadcast_in_dim.25), calls=%async_computation.1 | async-start | bytes 131072 | tf_op jit(solution)/shard_map/all_to_all | solution.py:187
  53.3 28.7 %collective-permute-start.4 = (s32[4,8,8,512]{3,2,1,0:T(8,128)S(1)}, s32[4,8,8,512]{3,2,1,0:T(8,128)S(1)}, u32[]{:S(2)}, u32[]{:S(2)}) collective-permute-start(s32[4,8,8,512]{3,2,1,0:T(8,128)S(1)} %dynamic-slice_bitcast_fusion), channel_id=1, source_target_pairs={{0,4},{4,0},{1,5},{5,1},{2,6},{6,2},{3,7},{7,3},{8,12},{12,8},{9,1... | collective-permute-start | bytes 1572872 | tf_op jit(solution)/shard_map/ppermute | solution.py:194
  62.1 1.2 collective-permute-start.1
  64.0 17.4 %all-to-all-start.2 = ((f32[128,1,128]{2,1,0:T(1,128)}), f32[128,1,128]{2,1,0:T(1,128)S(1)}, u32[]{:S(2)}, u32[]{:S(2)}) async-start(f32[128,1,128]{2,1,0:T(1,128)} %broadcast_in_dim.27), calls=%async_computation.2 | async-start | bytes 131072 | tf_op jit(solution)/shard_map/all_to_all | solution.py:187
  82.0 3.2 %collective-permute-start.2 = (f32[1,128]{1,0:T(1,128)S(1)}, f32[1,128]{1,0:T(1,128)S(1)}, u32[]{:S(2)}, u32[]{:S(2)}) collective-permute-start(f32[1,128]{1,0:T(1,128)S(1)} %get-tuple-element.33), channel_id=1, source_target_pairs={{0,4},{4,0},{1,5},{5,1},{2,6},{6,2},{3,7},{7,3},{8,12},{12,8},{9,1... | collective-permute-start | bytes 1544 | tf_op jit(solution)/shard_map/ppermute | solution.py:194
  83.3 20.3 %collective-permute-start.10 = (s32[2,4,8,512]{3,2,1,0:T(8,128)}, s32[2,4,8,512]{3,2,1,0:T(8,128)S(1)}, u32[]{:S(2)}, u32[]{:S(2)}) collective-permute-start(s32[2,4,8,512]{3,2,1,0:T(8,128)} %get-tuple-element.42), channel_id=1, source_target_pairs={{0,48},{8,56},{16,0},{24,8},{32,16},{40,24},{48,32},{56,40},{1,49}... | collective-permute-start | bytes 393224 | tf_op jit(solution)/shard_map/ppermute | solution.py:194
  84.4 23.7 %collective-permute-start.11 = (s32[2,4,8,512]{3,2,1,0:T(8,128)S(1)}, s32[2,4,8,512]{3,2,1,0:T(8,128)S(1)}, u32[]{:S(2)}, u32[]{:S(2)}) collective-permute-start(s32[2,4,8,512]{3,2,1,0:T(8,128)S(1)} %get-tuple-element.43), channel_id=1, source_target_pairs={{0,56},{8,0},{16,8},{24,16},{32,24},{40,32},{48,40},{56,48},{1,57}... | collective-permute-start | bytes 393224 | tf_op jit(solution)/shard_map/ppermute | solution.py:194
  85.8 22.8 %all-to-all-start.3 = ((f32[128,1,128]{2,1,0:T(1,128)}), f32[128,1,128]{2,1,0:T(1,128)S(1)}, u32[]{:S(2)}, u32[]{:S(2)}) async-start(f32[128,1,128]{2,1,0:T(1,128)} %broadcast_in_dim.29), calls=%async_computation.3 | async-start | bytes 131072 | tf_op jit(solution)/shard_map/all_to_all | solution.py:187
  97.7 21.4 %collective-permute-start.5 = (s32[2,4,8,512]{3,2,1,0:T(8,128)S(1)}, s32[2,4,8,512]{3,2,1,0:T(8,128)S(1)}, u32[]{:S(2)}, u32[]{:S(2)}) collective-permute-start(s32[2,4,8,512]{3,2,1,0:T(8,128)S(1)} %get-tuple-element.37), channel_id=1, source_target_pairs={{0,8},{8,16},{16,24},{24,32},{32,40},{40,48},{48,56},{56,0},{1,9},... | collective-permute-start | bytes 393224 | tf_op jit(solution)/shard_map/ppermute | solution.py:194
  99.4 19.7 %collective-permute-start.6 = (s32[2,4,8,512]{3,2,1,0:T(8,128)S(1)}, s32[2,4,8,512]{3,2,1,0:T(8,128)S(1)}, u32[]{:S(2)}, u32[]{:S(2)}) collective-permute-start(s32[2,4,8,512]{3,2,1,0:T(8,128)S(1)} %get-tuple-element.38), channel_id=1, source_target_pairs={{0,16},{8,24},{16,32},{24,40},{32,48},{40,56},{48,0},{56,8},{1,17}... | collective-permute-start | bytes 393224 | tf_op jit(solution)/shard_map/ppermute | solution.py:194
  103.0 17.8 %collective-permute-start.7 = (s32[2,4,8,512]{3,2,1,0:T(8,128)S(1)}, s32[2,4,8,512]{3,2,1,0:T(8,128)S(1)}, u32[]{:S(2)}, u32[]{:S(2)}) collective-permute-start(s32[2,4,8,512]{3,2,1,0:T(8,128)S(1)} %get-tuple-element.39), channel_id=1, source_target_pairs={{0,24},{8,32},{16,40},{24,48},{32,56},{40,0},{48,8},{56,16},{1,25}... | collective-permute-start | bytes 393224 | tf_op jit(solution)/shard_map/ppermute | solution.py:194
  103.6 24.9 %collective-permute-start.8 = (s32[2,4,8,512]{3,2,1,0:T(8,128)S(1)}, s32[2,4,8,512]{3,2,1,0:T(8,128)S(1)}, u32[]{:S(2)}, u32[]{:S(2)}) collective-permute-start(s32[2,4,8,512]{3,2,1,0:T(8,128)S(1)} %get-tuple-element.40), channel_id=1, source_target_pairs={{0,32},{8,40},{16,48},{24,56},{32,0},{40,8},{48,16},{56,24},{1,33}... | collective-permute-start | bytes 393224 | tf_op jit(solution)/shard_map/ppermute | solution.py:194
  108.1 20.4 %collective-permute-start.9 = (s32[2,4,8,512]{3,2,1,0:T(8,128)S(1)}, s32[2,4,8,512]{3,2,1,0:T(8,128)S(1)}, u32[]{:S(2)}, u32[]{:S(2)}) collective-permute-start(s32[2,4,8,512]{3,2,1,0:T(8,128)S(1)} %get-tuple-element.41), channel_id=1, source_target_pairs={{0,40},{8,48},{16,56},{24,0},{32,8},{40,16},{48,24},{56,32},{1,41}... | collective-permute-start | bytes 393224 | tf_op jit(solution)/shard_map/ppermute | solution.py:194
  109.7 24.0 %all-to-all-start.4 = ((f32[32,8,128]{2,1,0:T(8,128)}), f32[32,8,128]{2,1,0:T(8,128)S(1)}, u32[]{:S(2)}, u32[]{:S(2)}) async-start(f32[32,8,128]{2,1,0:T(8,128)} %get-tuple-element.35), calls=%async_computation.4 | async-start | bytes 262144 | tf_op jit(solution)/shard_map/all_to_all | solution.py:187
  129.1 9.7 %collective-permute-start.12 = (s32[8,2,8,512]{3,2,1,0:T(8,128)S(1)}, s32[8,2,8,512]{3,2,1,0:T(8,128)S(1)}, u32[]{:S(2)}, u32[]{:S(2)}) collective-permute-start(s32[8,2,8,512]{3,2,1,0:T(8,128)S(1)} %get-tuple-element.45), channel_id=1, source_target_pairs={{0,64},{64,128},{128,192},{192,0},{1,65},{65,129},{129,193},{193,1... | collective-permute-start | bytes 786440 | tf_op jit(solution)/shard_map/ppermute | solution.py:194
  129.5 13.9 %collective-permute-start.13 = (s32[8,2,8,512]{3,2,1,0:T(8,128)S(1)}, s32[8,2,8,512]{3,2,1,0:T(8,128)S(1)}, u32[]{:S(2)}, u32[]{:S(2)}) collective-permute-start(s32[8,2,8,512]{3,2,1,0:T(8,128)S(1)} %get-tuple-element.46), channel_id=1, source_target_pairs={{0,128},{64,192},{128,0},{192,64},{1,129},{65,193},{129,1},{193,65... | collective-permute-start | bytes 786440 | tf_op jit(solution)/shard_map/ppermute | solution.py:194
  133.3 10.1 %collective-permute-start.14 = (s32[8,2,8,512]{3,2,1,0:T(8,128)S(1)}, s32[8,2,8,512]{3,2,1,0:T(8,128)S(1)}, u32[]{:S(2)}, u32[]{:S(2)}) collective-permute-start(s32[8,2,8,512]{3,2,1,0:T(8,128)S(1)} %get-tuple-element.47), channel_id=1, source_target_pairs={{0,192},{64,0},{128,64},{192,128},{1,193},{65,1},{129,65},{193,129... | collective-permute-start | bytes 786440 | tf_op jit(solution)/shard_map/ppermute | solution.py:194
  133.7 13.7 %collective-permute-start.3 = (f32[32,8,128]{2,1,0:T(8,128)S(1)}, f32[32,8,128]{2,1,0:T(8,128)S(1)}, u32[]{:S(2)}, u32[]{:S(2)}) collective-permute-start(f32[32,8,128]{2,1,0:T(8,128)S(1)} %all-to-all-done.4.same_ref), channel_id=1, source_target_pairs={{0,4},{4,0},{1,5},{5,1},{2,6},{6,2},{3,7},{7,3},{8,12},{12,8},{9,1... | collective-permute-start | bytes 393224 | tf_op jit(solution)/shard_map/ppermute | solution.py:194
  143.4 4.1 %copy-start = (f32[8,32768]{1,0:T(8,128)S(1)}, f32[8,32768]{1,0:T(8,128)}, u32[]{:S(2)}) copy-start(f32[8,32768]{1,0:T(8,128)} %x_ref.1) | copy-start | bytes 3145732
